TPU v7x, 32 devices: a whole 2x2x4 slice. The times are simulated.
32 devices in a mesh: stage: 8 (over z, y), tp: 4 (over x, core).
Axes of the slice: x: 2, y: 2, z: 4, core: 2. Of those that a mesh axis runs over, the one named last changes fastest.
Arguments:
- x: bfloat16 [4, 512, 2048], P(None, 'tp')
- g: bfloat16 [8, 2, 2048], P('stage')
- w1: bfloat16 [8, 2, 2048, 8192], P('stage', None, None, 'tp')
- w2: bfloat16 [8, 2, 8192, 2048], P('stage', None, 'tp')
Outputs:
- output: bfloat16 [8, 4, 512, 2048], P('stage', None, 'tp')
All inputs are finite; a program needn't handle non-finite values.
Results may differ from a plain program's by a relative error of at most 0.02.
Values are sent between devices in bfloat16 or wider.
A program may use at most 1 GiB of HBM per device.

v0:
```python
import jax
import jax.numpy as jnp
from jax import lax
from jax.sharding import PartitionSpec as P

EPS = 1e-5


def _ln(y, g):
    yf = y.astype(jnp.float32)
    mu = jnp.mean(yf, axis=-1, keepdims=True)
    var = jnp.mean(jnp.square(yf - mu), axis=-1, keepdims=True)
    return ((yf - mu) * lax.rsqrt(var + EPS) * g.astype(jnp.float32)).astype(jnp.bfloat16)


def _block(y, g, w1, w2):
    h = lax.all_gather(_ln(y, g), 'tp', axis=0, tiled=True)
    a = jax.nn.gelu(jnp.dot(h, w1, preferred_element_type=jnp.float32)).astype(jnp.bfloat16)
    p = jnp.dot(a, w2, preferred_element_type=jnp.float32).astype(jnp.bfloat16)
    r = lax.psum_scatter(p, 'tp', scatter_dimension=0, tiled=True)
    return (y.astype(jnp.float32) + r.astype(jnp.float32)).astype(jnp.bfloat16)


def solution(mesh):
    S = mesh.shape['stage']
    fwd = [(i, i + 1) for i in range(S - 1)]

    def local(x, g, w1, w2):
        s = lax.axis_index('stage')
        M = x.shape[0]
        nb = g.shape[1]
        out = jnp.zeros_like(x)
        recv = jnp.zeros_like(x[0])
        for k in range(M + S - 1):
            y = jnp.where(s == 0, x[min(k, M - 1)], recv)
            for b in range(nb):
                y = _block(y, g[0, b], w1[0, b], w2[0, b])
            m = k - s
            mc = jnp.clip(m, 0, M - 1)
            old = lax.dynamic_index_in_dim(out, mc, 0, keepdims=False)
            out = lax.dynamic_update_index_in_dim(out, jnp.where((m >= 0) & (m < M), y, old), mc, 0)
            if k < M + S - 2:
                recv = lax.ppermute(y, 'stage', fwd)
        return out[None]

    return jax.shard_map(
        local, mesh=mesh,
        in_specs=(P(None, 'tp', None), P('stage', None, None),
                  P('stage', None, None, 'tp'), P('stage', None, 'tp', None)),
        out_specs=P('stage', None, 'tp', None), check_vma=False)
```

profile of v0, /device:TPU:29, one launch (start us, length us, event | category | flops | bytes accessed | tf_op | source)
XLA Modules:
  0.0 1794.8 jit_solution(7915496310681645492)
XLA Ops:
  12.0 23.7 %all-gather.23.cloned.1.call-done = bf16[512,2048]{1,0:T(8,128)(2,1)} async-done(((bf16[128,2048]{1,0:T(8,128)(2,1)}), bf16[512,2048]{1,0:T(8,128)(2,1)}) %all-gather.23.cloned.1.call-update) | async-done | bytes 2097168 | tf_op jit(solution)/shard_map/all_gather | solution.py:17
  35.8 16.5 fusion.264
  52.4 30.5 %reduce-scatter.23.cloned.1.call-done = bf16[128,2048]{1,0:T(8,128)(2,1)} async-done(((bf16[512,2048]{1,0:T(8,128)(2,1)}), bf16[128,2048]{1,0:T(8,128)(2,1)}) %reduce-scatter.23.cloned.1.call-update) | async-done | bytes 524304 | tf_op jit(solution)/shard_map/reduce_scatter | solution.py:20
  86.4 22.5 %all-gather.25.cloned.1.call-done = bf16[512,2048]{1,0:T(8,128)(2,1)} async-done(((bf16[128,2048]{1,0:T(8,128)(2,1)}), bf16[512,2048]{1,0:T(8,128)(2,1)}) %all-gather.25.cloned.1.call-update) | async-done | bytes 2097168 | tf_op jit(solution)/shard_map/all_gather | solution.py:17
  109.0 16.5 fusion.297
  125.6 30.5 %reduce-scatter.25.cloned.1.call-done = bf16[128,2048]{1,0:T(8,128)(2,1)} async-done(((bf16[512,2048]{1,0:T(8,128)(2,1)}), bf16[128,2048]{1,0:T(8,128)(2,1)}) %reduce-scatter.25.cloned.1.call-update) | async-done | bytes 524304 | tf_op jit(solution)/shard_map/reduce_scatter | solution.py:20
  175.1 24.0 %all-gather.27.cloned.1.call-done = bf16[512,2048]{1,0:T(8,128)(2,1)} async-done(((bf16[128,2048]{1,0:T(8,128)(2,1)}), bf16[512,2048]{1,0:T(8,128)(2,1)}) %all-gather.27.cloned.1.call-update) | async-done | bytes 2097168 | tf_op jit(solution)/shard_map/all_gather | solution.py:17
  199.1 16.5 fusion.267
  215.7 30.5 %reduce-scatter.27.cloned.1.call-done = bf16[128,2048]{1,0:T(8,128)(2,1)} async-done(((bf16[512,2048]{1,0:T(8,128)(2,1)}), bf16[128,2048]{1,0:T(8,128)(2,1)}) %reduce-scatter.27.cloned.1.call-update) | async-done | bytes 524304 | tf_op jit(solution)/shard_map/reduce_scatter | solution.py:20
  249.3 22.9 %all-gather.29.cloned.1.call-done = bf16[512,2048]{1,0:T(8,128)(2,1)} async-done(((bf16[128,2048]{1,0:T(8,128)(2,1)}), bf16[512,2048]{1,0:T(8,128)(2,1)}) %all-gather.29.cloned.1.call-update) | async-done | bytes 2097168 | tf_op jit(solution)/shard_map/all_gather | solution.py:17
  272.1 16.5 fusion.300
  288.8 30.5 %reduce-scatter.29.cloned.1.call-done = bf16[128,2048]{1,0:T(8,128)(2,1)} async-done(((bf16[512,2048]{1,0:T(8,128)(2,1)}), bf16[128,2048]{1,0:T(8,128)(2,1)}) %reduce-scatter.29.cloned.1.call-update) | async-done | bytes 524304 | tf_op jit(solution)/shard_map/reduce_scatter | solution.py:20
  338.1 23.9 %all-gather.31.cloned.1.call-done = bf16[512,2048]{1,0:T(8,128)(2,1)} async-done(((bf16[128,2048]{1,0:T(8,128)(2,1)}), bf16[512,2048]{1,0:T(8,128)(2,1)}) %all-gather.31.cloned.1.call-update) | async-done | bytes 2097168 | tf_op jit(solution)/shard_map/all_gather | solution.py:17
  362.0 16.5 fusion.270
  378.6 30.5 %reduce-scatter.31.cloned.1.call-done = bf16[128,2048]{1,0:T(8,128)(2,1)} async-done(((bf16[512,2048]{1,0:T(8,128)(2,1)}), bf16[128,2048]{1,0:T(8,128)(2,1)}) %reduce-scatter.31.cloned.1.call-update) | async-done | bytes 524304 | tf_op jit(solution)/shard_map/reduce_scatter | solution.py:20
  412.5 22.6 %all-gather.33.cloned.1.call-done = bf16[512,2048]{1,0:T(8,128)(2,1)} async-done(((bf16[128,2048]{1,0:T(8,128)(2,1)}), bf16[512,2048]{1,0:T(8,128)(2,1)}) %all-gather.33.cloned.1.call-update) | async-done | bytes 2097168 | tf_op jit(solution)/shard_map/all_gather | solution.py:17
  435.1 16.5 fusion.303
  451.7 30.5 %reduce-scatter.33.cloned.1.call-done = bf16[128,2048]{1,0:T(8,128)(2,1)} async-done(((bf16[512,2048]{1,0:T(8,128)(2,1)}), bf16[128,2048]{1,0:T(8,128)(2,1)}) %reduce-scatter.33.cloned.1.call-update) | async-done | bytes 524304 | tf_op jit(solution)/shard_map/reduce_scatter | solution.py:20
  501.0 24.0 %all-gather.35.cloned.1.call-done = bf16[512,2048]{1,0:T(8,128)(2,1)} async-done(((bf16[128,2048]{1,0:T(8,128)(2,1)}), bf16[512,2048]{1,0:T(8,128)(2,1)}) %all-gather.35.cloned.1.call-update) | async-done | bytes 2097168 | tf_op jit(solution)/shard_map/all_gather | solution.py:17
  525.0 16.5 fusion.273
  541.6 30.5 %reduce-scatter.35.cloned.1.call-done = bf16[128,2048]{1,0:T(8,128)(2,1)} async-done(((bf16[512,2048]{1,0:T(8,128)(2,1)}), bf16[128,2048]{1,0:T(8,128)(2,1)}) %reduce-scatter.35.cloned.1.call-update) | async-done | bytes 524304 | tf_op jit(solution)/shard_map/reduce_scatter | solution.py:20
  575.1 22.9 %all-gather.37.cloned.1.call-done = bf16[512,2048]{1,0:T(8,128)(2,1)} async-done(((bf16[128,2048]{1,0:T(8,128)(2,1)}), bf16[512,2048]{1,0:T(8,128)(2,1)}) %all-gather.37.cloned.1.call-update) | async-done | bytes 2097168 | tf_op jit(solution)/shard_map/all_gather | solution.py:17
  598.0 16.5 fusion.306
  614.7 30.5 %reduce-scatter.37.cloned.1.call-done = bf16[128,2048]{1,0:T(8,128)(2,1)} async-done(((bf16[512,2048]{1,0:T(8,128)(2,1)}), bf16[128,2048]{1,0:T(8,128)(2,1)}) %reduce-scatter.37.cloned.1.call-update) | async-done | bytes 524304 | tf_op jit(solution)/shard_map/reduce_scatter | solution.py:20
  664.0 23.9 %all-gather.39.cloned.1.call-done = bf16[512,2048]{1,0:T(8,128)(2,1)} async-done(((bf16[128,2048]{1,0:T(8,128)(2,1)}), bf16[512,2048]{1,0:T(8,128)(2,1)}) %all-gather.39.cloned.1.call-update) | async-done | bytes 2097168 | tf_op jit(solution)/shard_map/all_gather | solution.py:17
  687.9 16.5 fusion.276
  704.5 30.5 %reduce-scatter.39.cloned.1.call-done = bf16[128,2048]{1,0:T(8,128)(2,1)} async-done(((bf16[512,2048]{1,0:T(8,128)(2,1)}), bf16[128,2048]{1,0:T(8,128)(2,1)}) %reduce-scatter.39.cloned.1.call-update) | async-done | bytes 524304 | tf_op jit(solution)/shard_map/reduce_scatter | solution.py:20
  738.3 22.6 %all-gather.41.cloned.1.call-done = bf16[512,2048]{1,0:T(8,128)(2,1)} async-done(((bf16[128,2048]{1,0:T(8,128)(2,1)}), bf16[512,2048]{1,0:T(8,128)(2,1)}) %all-gather.41.cloned.1.call-update) | async-done | bytes 2097168 | tf_op jit(solution)/shard_map/all_gather | solution.py:17
  760.9 16.5 fusion.309
  777.6 30.5 %reduce-scatter.41.cloned.1.call-done = bf16[128,2048]{1,0:T(8,128)(2,1)} async-done(((bf16[512,2048]{1,0:T(8,128)(2,1)}), bf16[128,2048]{1,0:T(8,128)(2,1)}) %reduce-scatter.41.cloned.1.call-update) | async-done | bytes 524304 | tf_op jit(solution)/shard_map/reduce_scatter | solution.py:20
  826.8 24.0 %all-gather.43.cloned.1.call-done = bf16[512,2048]{1,0:T(8,128)(2,1)} async-done(((bf16[128,2048]{1,0:T(8,128)(2,1)}), bf16[512,2048]{1,0:T(8,128)(2,1)}) %all-gather.43.cloned.1.call-update) | async-done | bytes 2097168 | tf_op jit(solution)/shard_map/all_gather | solution.py:17
  850.8 16.5 fusion.279
  867.4 30.5 %reduce-scatter.43.cloned.1.call-done = bf16[128,2048]{1,0:T(8,128)(2,1)} async-done(((bf16[512,2048]{1,0:T(8,128)(2,1)}), bf16[128,2048]{1,0:T(8,128)(2,1)}) %reduce-scatter.43.cloned.1.call-update) | async-done | bytes 524304 | tf_op jit(solution)/shard_map/reduce_scatter | solution.py:20
  901.0 22.9 %all-gather.45.cloned.1.call-done = bf16[512,2048]{1,0:T(8,128)(2,1)} async-done(((bf16[128,2048]{1,0:T(8,128)(2,1)}), bf16[512,2048]{1,0:T(8,128)(2,1)}) %all-gather.45.cloned.1.call-update) | async-done | bytes 2097168 | tf_op jit(solution)/shard_map/all_gather | solution.py:17
  923.9 16.5 fusion.312
  940.5 30.5 %reduce-scatter.45.cloned.1.call-done = bf16[128,2048]{1,0:T(8,128)(2,1)} async-done(((bf16[512,2048]{1,0:T(8,128)(2,1)}), bf16[128,2048]{1,0:T(8,128)(2,1)}) %reduce-scatter.45.cloned.1.call-update) | async-done | bytes 524304 | tf_op jit(solution)/shard_map/reduce_scatter | solution.py:20
  989.9 23.9 %all-gather.47.cloned.1.call-done = bf16[512,2048]{1,0:T(8,128)(2,1)} async-done(((bf16[128,2048]{1,0:T(8,128)(2,1)}), bf16[512,2048]{1,0:T(8,128)(2,1)}) %all-gather.47.cloned.1.call-update) | async-done | bytes 2097168 | tf_op jit(solution)/shard_map/all_gather | solution.py:17
  1013.8 16.5 fusion.282
  1030.4 30.5 %reduce-scatter.47.cloned.1.call-done = bf16[128,2048]{1,0:T(8,128)(2,1)} async-done(((bf16[512,2048]{1,0:T(8,128)(2,1)}), bf16[128,2048]{1,0:T(8,128)(2,1)}) %reduce-scatter.47.cloned.1.call-update) | async-done | bytes 524304 | tf_op jit(solution)/shard_map/reduce_scatter | solution.py:20
  1064.2 22.6 %all-gather.49.cloned.1.call-done = bf16[512,2048]{1,0:T(8,128)(2,1)} async-done(((bf16[128,2048]{1,0:T(8,128)(2,1)}), bf16[512,2048]{1,0:T(8,128)(2,1)}) %all-gather.49.cloned.1.call-update) | async-done | bytes 2097168 | tf_op jit(solution)/shard_map/all_gather | solution.py:17
  1086.8 16.5 fusion.315
  1103.5 30.5 %reduce-scatter.49.cloned.1.call-done = bf16[128,2048]{1,0:T(8,128)(2,1)} async-done(((bf16[512,2048]{1,0:T(8,128)(2,1)}), bf16[128,2048]{1,0:T(8,128)(2,1)}) %reduce-scatter.49.cloned.1.call-update) | async-done | bytes 524304 | tf_op jit(solution)/shard_map/reduce_scatter | solution.py:20
  1152.7 24.0 %all-gather.51.cloned.1.call-done = bf16[512,2048]{1,0:T(8,128)(2,1)} async-done(((bf16[128,2048]{1,0:T(8,128)(2,1)}), bf16[512,2048]{1,0:T(8,128)(2,1)}) %all-gather.51.cloned.1.call-update) | async-done | bytes 2097168 | tf_op jit(solution)/shard_map/all_gather | solution.py:17
  1176.7 16.5 fusion.285
  1193.3 30.5 %reduce-scatter.51.cloned.1.call-done = bf16[128,2048]{1,0:T(8,128)(2,1)} async-done(((bf16[512,2048]{1,0:T(8,128)(2,1)}), bf16[128,2048]{1,0:T(8,128)(2,1)}) %reduce-scatter.51.cloned.1.call-update) | async-done | bytes 524304 | tf_op jit(solution)/shard_map/reduce_scatter | solution.py:20
  1226.9 22.9 %all-gather.53.cloned.1.call-done = bf16[512,2048]{1,0:T(8,128)(2,1)} async-done(((bf16[128,2048]{1,0:T(8,128)(2,1)}), bf16[512,2048]{1,0:T(8,128)(2,1)}) %all-gather.53.cloned.1.call-update) | async-done | bytes 2097168 | tf_op jit(solution)/shard_map/all_gather | solution.py:17
  1249.7 16.5 fusion.318
  1266.4 30.5 %reduce-scatter.53.cloned.1.call-done = bf16[128,2048]{1,0:T(8,128)(2,1)} async-done(((bf16[512,2048]{1,0:T(8,128)(2,1)}), bf16[128,2048]{1,0:T(8,128)(2,1)}) %reduce-scatter.53.cloned.1.call-update) | async-done | bytes 524304 | tf_op jit(solution)/shard_map/reduce_scatter | solution.py:20
  1315.7 23.9 %all-gather.55.cloned.1.call-done = bf16[512,2048]{1,0:T(8,128)(2,1)} async-done(((bf16[128,2048]{1,0:T(8,128)(2,1)}), bf16[512,2048]{1,0:T(8,128)(2,1)}) %all-gather.55.cloned.1.call-update) | async-done | bytes 2097168 | tf_op jit(solution)/shard_map/all_gather | solution.py:17
  1339.7 16.5 fusion.288
  1356.3 30.5 %reduce-scatter.55.cloned.1.call-done = bf16[128,2048]{1,0:T(8,128)(2,1)} async-done(((bf16[512,2048]{1,0:T(8,128)(2,1)}), bf16[128,2048]{1,0:T(8,128)(2,1)}) %reduce-scatter.55.cloned.1.call-update) | async-done | bytes 524304 | tf_op jit(solution)/shard_map/reduce_scatter | solution.py:20
  1390.1 22.6 %all-gather.57.cloned.1.call-done = bf16[512,2048]{1,0:T(8,128)(2,1)} async-done(((bf16[128,2048]{1,0:T(8,128)(2,1)}), bf16[512,2048]{1,0:T(8,128)(2,1)}) %all-gather.57.cloned.1.call-update) | async-done | bytes 2097168 | tf_op jit(solution)/shard_map/all_gather | solution.py:17
  1412.7 16.5 fusion.321
  1429.3 30.5 %reduce-scatter.57.cloned.1.call-done = bf16[128,2048]{1,0:T(8,128)(2,1)} async-done(((bf16[512,2048]{1,0:T(8,128)(2,1)}), bf16[128,2048]{1,0:T(8,128)(2,1)}) %reduce-scatter.57.cloned.1.call-update) | async-done | bytes 524304 | tf_op jit(solution)/shard_map/reduce_scatter | solution.py:20
  1478.6 24.0 %all-gather.59.cloned.1.call-done = bf16[512,2048]{1,0:T(8,128)(2,1)} async-done(((bf16[128,2048]{1,0:T(8,128)(2,1)}), bf16[512,2048]{1,0:T(8,128)(2,1)}) %all-gather.59.cloned.1.call-update) | async-done | bytes 2097168 | tf_op jit(solution)/shard_map/all_gather | solution.py:17
  1502.6 16.5 fusion.291
  1519.2 30.5 %reduce-scatter.59.cloned.1.call-done = bf16[128,2048]{1,0:T(8,128)(2,1)} async-done(((bf16[512,2048]{1,0:T(8,128)(2,1)}), bf16[128,2048]{1,0:T(8,128)(2,1)}) %reduce-scatter.59.cloned.1.call-update) | async-done | bytes 524304 | tf_op jit(solution)/shard_map/reduce_scatter | solution.py:20
  1552.8 22.9 %all-gather.61.cloned.1.call-done = bf16[512,2048]{1,0:T(8,128)(2,1)} async-done(((bf16[128,2048]{1,0:T(8,128)(2,1)}), bf16[512,2048]{1,0:T(8,128)(2,1)}) %all-gather.61.cloned.1.call-update) | async-done | bytes 2097168 | tf_op jit(solution)/shard_map/all_gather | solution.py:17
  1592.3 30.5 %reduce-scatter.61.cloned.1.call-done = bf16[128,2048]{1,0:T(8,128)(2,1)} async-done(((bf16[512,2048]{1,0:T(8,128)(2,1)}), bf16[128,2048]{1,0:T(8,128)(2,1)}) %reduce-scatter.61.cloned.1.call-update) | async-done | bytes 524304 | tf_op jit(solution)/shard_map/reduce_scatter | solution.py:20
  1641.6 23.9 %all-gather.63.cloned.1.call-done = bf16[512,2048]{1,0:T(8,128)(2,1)} async-done(((bf16[128,2048]{1,0:T(8,128)(2,1)}), bf16[512,2048]{1,0:T(8,128)(2,1)}) %all-gather.63.cloned.1.call-update) | async-done | bytes 2097168 | tf_op jit(solution)/shard_map/all_gather | solution.py:17
  1682.1 30.5 %reduce-scatter.63.cloned.1.call-done = bf16[128,2048]{1,0:T(8,128)(2,1)} async-done(((bf16[512,2048]{1,0:T(8,128)(2,1)}), bf16[128,2048]{1,0:T(8,128)(2,1)}) %reduce-scatter.63.cloned.1.call-update) | async-done | bytes 524304 | tf_op jit(solution)/shard_map/reduce_scatter | solution.py:20
  1715.8 22.8 %all-gather.65.cloned.1.call-done = bf16[512,2048]{1,0:T(8,128)(2,1)} async-done(((bf16[128,2048]{1,0:T(8,128)(2,1)}), bf16[512,2048]{1,0:T(8,128)(2,1)}) %all-gather.65.cloned.1.call-update) | async-done | bytes 2097168 | tf_op jit(solution)/shard_map/all_gather | solution.py:17
  1738.6 16.6 fusion.327
  1756.5 29.2 %reduce-scatter.65.cloned.1.call-done = bf16[128,2048]{1,0:T(8,128)(2,1)} async-done(((bf16[512,2048]{1,0:T(8,128)(2,1)}), bf16[128,2048]{1,0:T(8,128)(2,1)}) %reduce-scatter.65.cloned.1.call-update) | async-done | bytes 524304 | tf_op jit(solution)/shard_map/reduce_scatter | solution.py:20
  (243 shorter events, 266.4 us)
Async XLA Ops:
  6.5 29.2 %all-gather.23.cloned.1.call-start = ((), (), s32[]{:S(2)}) async-start(), calls=%async_computation.22 | async-start | bytes 2621440 | tf_op jit(solution)/shard_map/all_gather | solution.py:17
  12.0 70.9 %reduce-scatter.23.cloned.1.call-start = ((), (), s32[]{:S(2)}) async-start(), calls=%async_computation.23 | async-start | bytes 2621440 | tf_op jit(solution)/shard_map/reduce_scatter | solution.py:20
  52.3 56.7 %all-gather.25.cloned.1.call-start = ((), (), s32[]{:S(2)}) async-start(), calls=%async_computation.24 | async-start | bytes 2621440 | tf_op jit(solution)/shard_map/all_gather | solution.py:17
  85.9 70.2 %reduce-scatter.25.cloned.1.call-start = ((), (), s32[]{:S(2)}) async-start(), calls=%async_computation.25 | async-start | bytes 2621440 | tf_op jit(solution)/shard_map/reduce_scatter | solution.py:20
  125.5 73.5 %all-gather.27.cloned.1.call-start = ((), (), s32[]{:S(2)}) async-start(), calls=%async_computation.26 | async-start | bytes 2621440 | tf_op jit(solution)/shard_map/all_gather | solution.py:17
  157.6 14.5 collective-permute-start
  174.9 71.3 %reduce-scatter.27.cloned.1.call-start = ((), (), s32[]{:S(2)}) async-start(), calls=%async_computation.27 | async-start | bytes 2621440 | tf_op jit(solution)/shard_map/reduce_scatter | solution.py:20
  215.6 56.5 %all-gather.29.cloned.1.call-start = ((), (), s32[]{:S(2)}) async-start(), calls=%async_computation.28 | async-start | bytes 2621440 | tf_op jit(solution)/shard_map/all_gather | solution.py:17
  249.0 70.2 %reduce-scatter.29.cloned.1.call-start = ((), (), s32[]{:S(2)}) async-start(), calls=%async_computation.29 | async-start | bytes 2621440 | tf_op jit(solution)/shard_map/reduce_scatter | solution.py:20
  288.7 73.4 %all-gather.31.cloned.1.call-start = ((), (), s32[]{:S(2)}) async-start(), calls=%async_computation.30 | async-start | bytes 2621440 | tf_op jit(solution)/shard_map/all_gather | solution.py:17
  320.6 14.5 collective-permute-start.1
  337.8 71.3 %reduce-scatter.31.cloned.1.call-start = ((), (), s32[]{:S(2)}) async-start(), calls=%async_computation.31 | async-start | bytes 2621440 | tf_op jit(solution)/shard_map/reduce_scatter | solution.py:20
  378.6 56.5 %all-gather.33.cloned.1.call-start = ((), (), s32[]{:S(2)}) async-start(), calls=%async_computation.32 | async-start | bytes 2621440 | tf_op jit(solution)/shard_map/all_gather | solution.py:17
  411.9 70.2 %reduce-scatter.33.cloned.1.call-start = ((), (), s32[]{:S(2)}) async-start(), calls=%async_computation.33 | async-start | bytes 2621440 | tf_op jit(solution)/shard_map/reduce_scatter | solution.py:20
  451.6 73.4 %all-gather.35.cloned.1.call-start = ((), (), s32[]{:S(2)}) async-start(), calls=%async_computation.34 | async-start | bytes 2621440 | tf_op jit(solution)/shard_map/all_gather | solution.py:17
  483.5 14.5 collective-permute-start.2
  500.7 71.3 %reduce-scatter.35.cloned.1.call-start = ((), (), s32[]{:S(2)}) async-start(), calls=%async_computation.35 | async-start | bytes 2621440 | tf_op jit(solution)/shard_map/reduce_scatter | solution.py:20
  541.5 56.5 %all-gather.37.cloned.1.call-start = ((), (), s32[]{:S(2)}) async-start(), calls=%async_computation.36 | async-start | bytes 2621440 | tf_op jit(solution)/shard_map/all_gather | solution.py:17
  574.9 70.2 %reduce-scatter.37.cloned.1.call-start = ((), (), s32[]{:S(2)}) async-start(), calls=%async_computation.37 | async-start | bytes 2621440 | tf_op jit(solution)/shard_map/reduce_scatter | solution.py:20
  614.5 73.4 %all-gather.39.cloned.1.call-start = ((), (), s32[]{:S(2)}) async-start(), calls=%async_computation.38 | async-start | bytes 2621440 | tf_op jit(solution)/shard_map/all_gather | solution.py:17
  646.5 14.5 collective-permute-start.3
  663.7 71.3 %reduce-scatter.39.cloned.1.call-start = ((), (), s32[]{:S(2)}) async-start(), calls=%async_computation.39 | async-start | bytes 2621440 | tf_op jit(solution)/shard_map/reduce_scatter | solution.py:20
  704.5 56.5 %all-gather.41.cloned.1.call-start = ((), (), s32[]{:S(2)}) async-start(), calls=%async_computation.40 | async-start | bytes 2621440 | tf_op jit(solution)/shard_map/all_gather | solution.py:17
  737.8 70.2 %reduce-scatter.41.cloned.1.call-start = ((), (), s32[]{:S(2)}) async-start(), calls=%async_computation.41 | async-start | bytes 2621440 | tf_op jit(solution)/shard_map/reduce_scatter | solution.py:20
  777.5 73.4 %all-gather.43.cloned.1.call-start = ((), (), s32[]{:S(2)}) async-start(), calls=%async_computation.42 | async-start | bytes 2621440 | tf_op jit(solution)/shard_map/all_gather | solution.py:17
  809.4 14.5 collective-permute-start.4
  826.6 71.3 %reduce-scatter.43.cloned.1.call-start = ((), (), s32[]{:S(2)}) async-start(), calls=%async_computation.43 | async-start | bytes 2621440 | tf_op jit(solution)/shard_map/reduce_scatter | solution.py:20
  867.4 56.5 %all-gather.45.cloned.1.call-start = ((), (), s32[]{:S(2)}) async-start(), calls=%async_computation.44 | async-start | bytes 2621440 | tf_op jit(solution)/shard_map/all_gather | solution.py:17
  900.8 70.2 %reduce-scatter.45.cloned.1.call-start = ((), (), s32[]{:S(2)}) async-start(), calls=%async_computation.45 | async-start | bytes 2621440 | tf_op jit(solution)/shard_map/reduce_scatter | solution.py:20
  940.4 73.4 %all-gather.47.cloned.1.call-start = ((), (), s32[]{:S(2)}) async-start(), calls=%async_computation.46 | async-start | bytes 2621440 | tf_op jit(solution)/shard_map/all_gather | solution.py:17
  972.3 14.5 collective-permute-start.5
  989.6 71.3 %reduce-scatter.47.cloned.1.call-start = ((), (), s32[]{:S(2)}) async-start(), calls=%async_computation.47 | async-start | bytes 2621440 | tf_op jit(solution)/shard_map/reduce_scatter | solution.py:20
  1030.3 56.5 %all-gather.49.cloned.1.call-start = ((), (), s32[]{:S(2)}) async-start(), calls=%async_computation.48 | async-start | bytes 2621440 | tf_op jit(solution)/shard_map/all_gather | solution.py:17
  1063.7 70.2 %reduce-scatter.49.cloned.1.call-start = ((), (), s32[]{:S(2)}) async-start(), calls=%async_computation.49 | async-start | bytes 2621440 | tf_op jit(solution)/shard_map/reduce_scatter | solution.py:20
  1103.4 73.4 %all-gather.51.cloned.1.call-start = ((), (), s32[]{:S(2)}) async-start(), calls=%async_computation.50 | async-start | bytes 2621440 | tf_op jit(solution)/shard_map/all_gather | solution.py:17
  1135.3 14.5 collective-permute-start.6
  1152.5 71.3 %reduce-scatter.51.cloned.1.call-start = ((), (), s32[]{:S(2)}) async-start(), calls=%async_computation.51 | async-start | bytes 2621440 | tf_op jit(solution)/shard_map/reduce_scatter | solution.py:20
  1193.3 56.5 %all-gather.53.cloned.1.call-start = ((), (), s32[]{:S(2)}) async-start(), calls=%async_computation.52 | async-start | bytes 2621440 | tf_op jit(solution)/shard_map/all_gather | solution.py:17
  1226.6 70.2 %reduce-scatter.53.cloned.1.call-start = ((), (), s32[]{:S(2)}) async-start(), calls=%async_computation.53 | async-start | bytes 2621440 | tf_op jit(solution)/shard_map/reduce_scatter | solution.py:20
  1266.3 73.4 %all-gather.55.cloned.1.call-start = ((), (), s32[]{:S(2)}) async-start(), calls=%async_computation.54 | async-start | bytes 2621440 | tf_op jit(solution)/shard_map/all_gather | solution.py:17
  1298.2 14.5 collective-permute-start.7
  1315.4 71.3 %reduce-scatter.55.cloned.1.call-start = ((), (), s32[]{:S(2)}) async-start(), calls=%async_computation.55 | async-start | bytes 2621440 | tf_op jit(solution)/shard_map/reduce_scatter | solution.py:20
  1356.2 56.5 %all-gather.57.cloned.1.call-start = ((), (), s32[]{:S(2)}) async-start(), calls=%async_computation.56 | async-start | bytes 2621440 | tf_op jit(solution)/shard_map/all_gather | solution.py:17
  1389.6 70.2 %reduce-scatter.57.cloned.1.call-start = ((), (), s32[]{:S(2)}) async-start(), calls=%async_computation.57 | async-start | bytes 2621440 | tf_op jit(solution)/shard_map/reduce_scatter | solution.py:20
  1429.2 73.4 %all-gather.59.cloned.1.call-start = ((), (), s32[]{:S(2)}) async-start(), calls=%async_computation.58 | async-start | bytes 2621440 | tf_op jit(solution)/shard_map/all_gather | solution.py:17
  1461.1 14.5 collective-permute-start.8
  1478.4 71.3 %reduce-scatter.59.cloned.1.call-start = ((), (), s32[]{:S(2)}) async-start(), calls=%async_computation.59 | async-start | bytes 2621440 | tf_op jit(solution)/shard_map/reduce_scatter | solution.py:20
  1519.2 56.5 %all-gather.61.cloned.1.call-start = ((), (), s32[]{:S(2)}) async-start(), calls=%async_computation.60 | async-start | bytes 2621440 | tf_op jit(solution)/shard_map/all_gather | solution.py:17
  1552.5 70.2 %reduce-scatter.61.cloned.1.call-start = ((), (), s32[]{:S(2)}) async-start(), calls=%async_computation.61 | async-start | bytes 2621440 | tf_op jit(solution)/shard_map/reduce_scatter | solution.py:20
  1592.2 73.4 %all-gather.63.cloned.1.call-start = ((), (), s32[]{:S(2)}) async-start(), calls=%async_computation.62 | async-start | bytes 2621440 | tf_op jit(solution)/shard_map/all_gather | solution.py:17
  1624.1 14.5 collective-permute-start.9
  1641.3 71.3 %reduce-scatter.63.cloned.1.call-start = ((), (), s32[]{:S(2)}) async-start(), calls=%async_computation.63 | async-start | bytes 2621440 | tf_op jit(solution)/shard_map/reduce_scatter | solution.py:20
  1682.1 56.5 %all-gather.65.cloned.1.call-start = ((), (), s32[]{:S(2)}) async-start(), calls=%async_computation.64 | async-start | bytes 2621440 | tf_op jit(solution)/shard_map/all_gather | solution.py:17
  1715.5 70.3 %reduce-scatter.65.cloned.1.call-start = ((), (), s32[]{:S(2)}) async-start(), calls=%async_computation.65 | async-start | bytes 2621440 | tf_op jit(solution)/shard_map/reduce_scatter | solution.py:20
Sparse Core Ops, SparseCore 0:
  12.1 23.6 all-gather.22
  52.4 30.4 reduce-scatter.22
  86.0 22.9 all-gather.24
  125.7 30.4 reduce-scatter.24
  175.0 24.0 all-gather.26
  215.8 30.4 reduce-scatter.26
  249.1 22.9 all-gather.28
  288.8 30.4 reduce-scatter.28
  337.9 24.0 all-gather.30
  378.7 30.4 reduce-scatter.30
  412.1 22.9 all-gather.32
  451.7 30.4 reduce-scatter.32
  500.9 24.0 all-gather.34
  541.6 30.4 reduce-scatter.34
  575.0 22.9 all-gather.36
  614.7 30.4 reduce-scatter.36
  663.8 24.0 all-gather.38
  704.6 30.4 reduce-scatter.38
  737.9 22.9 all-gather.40
  777.6 30.4 reduce-scatter.40
  826.7 24.0 all-gather.42
  867.5 30.4 reduce-scatter.42
  900.9 22.9 all-gather.44
  940.5 30.4 reduce-scatter.44
  989.7 24.0 all-gather.46
  1030.5 30.4 reduce-scatter.46
  1063.8 22.9 all-gather.48
  1103.5 30.4 reduce-scatter.48
  1152.6 24.0 all-gather.50
  1193.4 30.4 reduce-scatter.50
  1226.8 22.9 all-gather.52
  1266.4 30.4 reduce-scatter.52
  1315.6 24.0 all-gather.54
  1356.3 30.4 reduce-scatter.54
  1389.7 22.9 all-gather.56
  1429.4 30.4 reduce-scatter.56
  1478.5 24.0 all-gather.58
  1519.3 30.4 reduce-scatter.58
  1552.6 22.9 all-gather.60
  1592.3 30.4 reduce-scatter.60
  1641.4 24.0 all-gather.62
  1682.2 30.4 reduce-scatter.62
  1715.6 22.9 all-gather.64
  1755.3 30.4 reduce-scatter.64
where the time goes:
time: 1800 us; the launch traced here: 1790 us
  waiting for transfers between devices  1320 us (73%)
  matrix products  364 us (20%)
  other arithmetic  78.6 us (4%)
  starting transfers between devices  20.6 us (1%)
    reduce_scatter x22, waiting for transfers between devices, _block(): r = lax.psum_scatter(p, 'tp', scatter_dimension=0, tiled=True)  670 us
    all_gather x22, waiting for transfers between devices, _block(): h = lax.all_gather(_ln(y, g), 'tp', axis=0, tiled=True)  513 us
    dot_general x22, matrix products, _block(): p = jnp.dot(a, w2, preferred_element_type=jnp.float32).astype(jnp.bfloat16)  364 us
    ppermute x10, waiting for transfers between devices, local(): recv = lax.ppermute(y, 'stage', fwd)  132 us
  transfers between devices with their start and end apart: 54, of which 54 were waited for; matrix products, arithmetic and copies ran while one was open for 0% of the time, Pallas kernels for 0%

commit v1 on v0

v1 whole, which is shorter than its diff:
```python
import functools

import jax
import jax.numpy as jnp
from jax import lax
from jax.experimental import pallas as pl
from jax.experimental.pallas import tpu as pltpu
from jax.sharding import PartitionSpec as P

EPS = 1e-5
CHUNK = 64
PIECES = 4
MESH = pl.DeviceIdType.MESH
F32, BF16 = jnp.float32, jnp.bfloat16


def _gelu(v):
    return 0.5 * v * (1.0 + jnp.tanh(0.7978845608028654 * (v + 0.044715 * (v * v * v))))


def _kernel(S, M, TL, x_ref, g_ref, w1_ref, w2_ref, out_ref, W1, W2, y, xr, p, h, a,
            w_sem, w_send, y_sem, y_send, x_sem, p_send, o_sem, o_send, in_send):
    C = CHUNK
    s, r = lax.axis_index('stage'), lax.axis_index('tp')
    xp, c = r // 2, r % 2
    sub_n = TL // C
    per_rank = M * sub_n
    N = 4 * per_rank
    D = h.shape[1]
    DP = D // PIECES
    H = W1.shape[2]
    TH = min(512, H)
    sib = (s, 2 * xp + 1 - c)
    partner = (s, 2 * (1 - xp) + c)
    succ = (s + c, 2 * xp + 1 - c)
    has_succ = 2 * s + c < 2 * S - 1

    def remote(src, dst, ss, rs, dev):
        return pltpu.make_async_remote_copy(src_ref=src, dst_ref=dst, send_sem=ss, recv_sem=rs,
                                            device_id=dev, device_id_type=MESH)

    own1 = pltpu.make_async_copy(w1_ref.at[0, c], W1.at[0], w_sem.at[0])
    own2 = pltpu.make_async_copy(w2_ref.at[0, c], W2.at[0], w_sem.at[2])
    sib1 = remote(w1_ref.at[0, 1 - c], W1.at[1], w_send.at[0], w_sem.at[1], sib)
    sib2 = remote(w2_ref.at[0, 1 - c], W2.at[1], w_send.at[1], w_sem.at[3], sib)
    own1.start()

    def x_piece(i, k):
        return x_ref.at[i // sub_n, pl.ds(pl.multiple_of((i % sub_n) * C, C), C), pl.ds(k * DP, DP)]

    def sender(i):
        return jnp.maximum(1, i * S // per_rank)

    @pl.when(s == 0)
    def _():
        @pl.loop(0, per_rank)
        def _(i):
            for k in range(PIECES):
                @pl.when(c == 0)
                def _():
                    pltpu.make_async_copy(x_piece(i, k), y.at[4 * i + r, k], y_sem.at[4 * i + r]).start()

                @pl.when(c == 1)
                def _():
                    remote(x_piece(i, k), y.at[4 * i + r, k], in_send.at[i], y_sem.at[4 * i + r], sib).start()

    @pl.when(s > 0)
    def _():
        @pl.loop(0, per_rank)
        def _(i):
            @pl.when(s == sender(i))
            def _():
                for k in range(PIECES):
                    remote(x_piece(i, k), y.at[4 * i + r, k], in_send.at[i], y_sem.at[4 * i + r],
                           (0, 2 * (1 - xp))).start()

    sib1.start()
    own2.start()
    sib2.start()

    g = jnp.where(c == 0, g_ref[0, 0:1, :].astype(F32), g_ref[0, 1:2, :].astype(F32))

    def p_copy(t, k):
        return remote(p.at[t % 2, k], xr.at[t, k], p_send.at[t % 2, k], x_sem.at[t, k], partner)

    def out_piece(t, k):
        i = t // 4
        return out_ref.at[0, i // sub_n, pl.ds(pl.multiple_of((i % sub_n) * C, C), C), pl.ds(k * DP, DP)]

    def finish(t, k):
        p_copy(t, k).wait()
        v = y[t, k].astype(F32) + (p[t % 2, k].astype(F32) + xr[t, k].astype(F32))
        y[t, k] = v.astype(BF16)

        @pl.when(has_succ)
        def _():
            remote(y.at[t, k], y.at[t, k], y_send.at[t], y_sem.at[t], succ).start()

        mine = (c == 1) & ((t % 4) // 2 == xp)

        @pl.when(mine & (t % 2 == 1))
        def _():
            pltpu.make_async_copy(y.at[t, k], out_piece(t, k), o_sem.at[t // 4]).start()

        @pl.when(mine & (t % 2 == 0))
        def _():
            remote(y.at[t, k], out_piece(t, k), o_send.at[t // 4], o_sem.at[t // 4], sib).start()

    def step(t, first):
        pltpu.make_async_copy(y.at[t], y.at[t], y_sem.at[t]).wait()
        tot = y[t, 0].astype(F32)
        for k in range(1, PIECES):
            tot = tot + y[t, k].astype(F32)
        mu = jnp.sum(tot, axis=-1, keepdims=True) * (1.0 / D)
        sq = None
        for k in range(PIECES):
            d = y[t, k].astype(F32) - mu
            sq = d * d if sq is None else sq + d * d
        rstd = lax.rsqrt(jnp.sum(sq, axis=-1, keepdims=True) * (1.0 / D) + EPS)
        for k in range(PIECES):
            cols = slice(k * DP, (k + 1) * DP)
            h[:, cols] = ((y[t, k].astype(F32) - mu) * rstd * g[:, cols]).astype(BF16)
        if first:
            own1.wait()
        for half in range(2):
            if first and half == 1:
                sib1.wait_recv()
            for j in range(H // TH):
                acc = jnp.dot(h[...], W1[half, :, j * TH:(j + 1) * TH], preferred_element_type=F32)
                a[:, half * H + j * TH:half * H + (j + 1) * TH] = _gelu(acc).astype(BF16)
        if first:
            own2.wait()
            sib2.wait_recv()
        for k in range(PIECES):
            if not first:
                finish(t - 1, k)
            cols = slice(k * DP, (k + 1) * DP)
            acc = jnp.dot(a[:, :H], W2[0, :, cols], preferred_element_type=F32)
            acc = acc + jnp.dot(a[:, H:], W2[1, :, cols], preferred_element_type=F32)
            p[t % 2, k] = acc.astype(BF16)
            p_copy(t, k).start()

    step(0, True)

    @pl.loop(1, N)
    def _(t):
        step(t, False)

    for k in range(PIECES):
        finish(N - 1, k)

    sib1.wait_send()
    sib2.wait_send()

    @pl.when(has_succ)
    def _():
        @pl.loop(0, N)
        def _(t):
            remote(y.at[t], y.at[t], y_send.at[t], y_sem.at[t], succ).wait_send()

    @pl.loop(0, per_rank)
    def _(i):
        pltpu.make_async_copy(y.at[i], y.at[i], o_sem.at[i]).wait()

        @pl.when(c == 1)
        def _():
            pltpu.make_async_copy(y.at[i], y.at[i], o_send.at[i]).wait()

        @pl.when((s == sender(i)) | ((s == 0) & (c == 1)))
        def _():
            pltpu.make_async_copy(y.at[i], y.at[i], in_send.at[i]).wait()


def solution(mesh):
    S = mesh.shape['stage']

    def local(x, g, w1, w2):
        M, TL, D = x.shape
        H = w1.shape[-1]
        N = 4 * M * (TL // CHUNK)
        DP = D // PIECES
        dma = pltpu.SemaphoreType.DMA
        return pl.pallas_call(
            functools.partial(_kernel, S, M, TL),
            out_shape=jax.ShapeDtypeStruct((1, M, TL, D), BF16),
            in_specs=[pl.BlockSpec(memory_space=pl.ANY), pl.BlockSpec(memory_space=pltpu.VMEM),
                      pl.BlockSpec(memory_space=pl.ANY), pl.BlockSpec(memory_space=pl.ANY)],
            out_specs=pl.BlockSpec(memory_space=pl.ANY),
            scratch_shapes=[
                pltpu.VMEM((2, D, H), BF16), pltpu.VMEM((2, H, D), BF16),
                pltpu.VMEM((N, PIECES, CHUNK, DP), BF16), pltpu.VMEM((N, PIECES, CHUNK, DP), BF16),
                pltpu.VMEM((2, PIECES, CHUNK, DP), BF16), pltpu.VMEM((CHUNK, D), BF16),
                pltpu.VMEM((CHUNK, 2 * H), BF16),
                dma((4,)), dma((2,)), dma((N,)), dma((N,)), dma((N, PIECES)), dma((2, PIECES)),
                dma((N // 4,)), dma((N // 4,)), dma((N // 4,)),
            ],
            compiler_params=pltpu.CompilerParams(has_side_effects=True, vmem_limit_bytes=67043328),
        )(x, g, w1, w2)

    return jax.shard_map(
        local, mesh=mesh,
        in_specs=(P(None, 'tp', None), P('stage', None, None),
                  P('stage', None, None, 'tp'), P('stage', None, 'tp', None)),
        out_specs=P('stage', None, 'tp', None), check_vma=False)
```

time: 1800 us -> 478 us (0.27)
  waiting for transfers between devices: 1320 us -> 0 us
  Pallas kernels: 0 us -> 474 us
  matrix products: 364 us -> 0 us
  other arithmetic: 78.6 us -> 0 us
  starting transfers between devices: 20.6 us -> 0 us
    reduce_scatter x22 -> x0, waiting for transfers between devices: 670 us -> none  [_block(): r = lax.psum_scatter(p, 'tp', scatter_dimension=0, tiled=True)]
    all_gather x22 -> x0, waiting for transfers between devices: 513 us -> none  [_block(): h = lax.all_gather(_ln(y, g), 'tp', axis=0, tiled=True)]
    pallas_call x0 -> x1, Pallas kernels: none -> 474 us  [local(): pl.pallas_call(functools.partial(_kernel, S, M, TL), out_shape=jax.ShapeD...]
    dot_general x22 -> x0, matrix products: 364 us -> none  [_block(): p = jnp.dot(a, w2, preferred_element_type=jnp.float32).astype(jnp.bfloat16)]
    ppermute x10 -> x0, waiting for transfers between devices: 132 us -> none  [local(): recv = lax.ppermute(y, 'stage', fwd)]
    reduce_sum x44 -> x0, other arithmetic: 35.7 us -> none  [the longest x22 28.3 us: _ln(): mu = jnp.mean(yf, axis=-1, keepdims=True)]
    convert_element_type x23 -> x0, other arithmetic: 27.4 us -> none  [the longest x22 26.6 us: _ln(): ((yf - mu) * lax.rsqrt(var + EPS) * g.astype(jnp.float32)).astype(jnp.bfl...]
  transfers between devices with their start and end apart: 54 -> 0, of which waited for: 54 -> 0; matrix products, arithmetic and copies ran while one was open for 0% -> 0% of each run, Pallas kernels for 0% -> 0%
where the time goes in v1:
time: 478 us
  Pallas kernels  474 us (99%)
    pallas_call x1, Pallas kernels, local(): pl.pallas_call(functools.partial(_kernel, S, M, TL), out_shape=jax.ShapeD...  474 us

profile of v1, /device:TPU:29, one launch (start us, length us, event | category | flops | bytes accessed | tf_op | source)
XLA Modules:
  0.0 477.6 jit_solution(7887994958148507015)
XLA Ops:
  0.0 474.4 %shard_map.46 = bf16[1,4,128,2048]{3,2,1,0:T(8,128)(2,1)} custom-call(bf16[4,128,2048]{2,1,0:T(8,128)(2,1)} %x_ref.1, bf16[1,2,2048]{2,1,0:T(2,128)(2,1)} %g_ref.1, bf16[1,2,2048,2048]{3,2,1,0:T(8,128)(2,1)} %w1_ref.1, bf16[1,2,2048,2048]{3,2,1,0:T(8,128)(2,1)} %w2_ref.1), custom_call_target="tpu_custom_call" | custom-call | tf_op jit(solution)/shard_map/pallas_call | solution.py:183
  474.4 3.2 copy.6

commit v2 on v1

--- a/solution.py
+++ b/solution.py
@@ -9,7 +9,9 @@
 
 EPS = 1e-5
 CHUNK = 64
+ROWS = 128
 PIECES = 4
+ORDER = ('A0', 'A1', 'A2', 'A3', 'F0', 'F1', 'F2', 'T0', 'F3', 'T1', 'T2', 'T3')
 MESH = pl.DeviceIdType.MESH
 F32, BF16 = jnp.float32, jnp.bfloat16
 
@@ -29,7 +31,7 @@
     D = h.shape[1]
     DP = D // PIECES
     H = W1.shape[2]
-    TH = min(512, H)
+    TH = min(512, H // 2)
     sib = (s, 2 * xp + 1 - c)
     partner = (s, 2 * (1 - xp) + c)
     succ = (s + c, 2 * xp + 1 - c)
@@ -88,7 +90,8 @@
         return out_ref.at[0, i // sub_n, pl.ds(pl.multiple_of((i % sub_n) * C, C), C), pl.ds(k * DP, DP)]
 
     def finish(t, k):
-        p_copy(t, k).wait()
+        copy = p_copy(t, k)
+        copy.wait_recv()
         v = y[t, k].astype(F32) + (p[t % 2, k].astype(F32) + xr[t, k].astype(F32))
         y[t, k] = v.astype(BF16)
 
@@ -96,15 +99,20 @@
         def _():
             remote(y.at[t, k], y.at[t, k], y_send.at[t], y_sem.at[t], succ).start()
 
+        copy.wait_send()
+
+    def put_out(t):
         mine = (c == 1) & ((t % 4) // 2 == xp)
 
         @pl.when(mine & (t % 2 == 1))
         def _():
-            pltpu.make_async_copy(y.at[t, k], out_piece(t, k), o_sem.at[t // 4]).start()
+            for k in range(PIECES):
+                pltpu.make_async_copy(y.at[t, k], out_piece(t, k), o_sem.at[t // 4]).start()
 
         @pl.when(mine & (t % 2 == 0))
         def _():
-            remote(y.at[t, k], out_piece(t, k), o_send.at[t // 4], o_sem.at[t // 4], sib).start()
+            for k in range(PIECES):
+                remote(y.at[t, k], out_piece(t, k), o_send.at[t // 4], o_sem.at[t // 4], sib).start()
 
     def step(t, first):
         pltpu.make_async_copy(y.at[t], y.at[t], y_sem.at[t]).wait()
@@ -119,27 +127,38 @@
         rstd = lax.rsqrt(jnp.sum(sq, axis=-1, keepdims=True) * (1.0 / D) + EPS)
         for k in range(PIECES):
             cols = slice(k * DP, (k + 1) * DP)
-            h[:, cols] = ((y[t, k].astype(F32) - mu) * rstd * g[:, cols]).astype(BF16)
-        if first:
-            own1.wait()
-        for half in range(2):
-            if first and half == 1:
-                sib1.wait_recv()
-            for j in range(H // TH):
-                acc = jnp.dot(h[...], W1[half, :, j * TH:(j + 1) * TH], preferred_element_type=F32)
-                a[:, half * H + j * TH:half * H + (j + 1) * TH] = _gelu(acc).astype(BF16)
-        if first:
-            own2.wait()
-            sib2.wait_recv()
-        for k in range(PIECES):
-            if not first:
-                finish(t - 1, k)
-            cols = slice(k * DP, (k + 1) * DP)
-            acc = jnp.dot(a[:, :H], W2[0, :, cols], preferred_element_type=F32)
-            acc = acc + jnp.dot(a[:, H:], W2[1, :, cols], preferred_element_type=F32)
-            p[t % 2, k] = acc.astype(BF16)
-            p_copy(t, k).start()
-
+            h[:C, cols] = ((y[t, k].astype(F32) - mu) * rstd * g[:, cols]).astype(BF16)
+        for op in ORDER:
+            kind, k = op[0], int(op[1:])
+            if kind == 'A':
+                if first and k == 0:
+                    own1.wait()
+                if first and k == 2:
+                    sib1.wait_recv()
+                Q = H // 2
+                for j in range(0, Q, TH):
+                    o = (k % 2) * Q + j
+                    acc = jnp.dot(h[...], W1[k // 2, :, o:o + TH], preferred_element_type=F32)
+                    a[:C, k * Q + j:k * Q + j + TH] = _gelu(acc[:C]).astype(BF16)
+            elif kind == 'F':
+                if not first:
+                    finish(t - 1, k)
+            else:
+                if first and k == 0:
+                    own2.wait()
+                    sib2.wait_recv()
+                TN = min(512, DP)
+                for j in range(0, DP, TN):
+                    o = k * DP + j
+                    acc = jnp.dot(a[:, :H], W2[0, :, o:o + TN], preferred_element_type=F32)
+                    acc = acc + jnp.dot(a[:, H:], W2[1, :, o:o + TN], preferred_element_type=F32)
+                    p[t % 2, k, :, j:j + TN] = acc[:C].astype(BF16)
+                p_copy(t, k).start()
+        if not first:
+            put_out(t - 1)
+
+    h[C:, :] = jnp.zeros((ROWS - C, D), BF16)
+    a[C:, :] = jnp.zeros((ROWS - C, 2 * H), BF16)
     step(0, True)
 
     @pl.loop(1, N)
@@ -148,6 +167,7 @@
 
     for k in range(PIECES):
         finish(N - 1, k)
+    put_out(N - 1)
 
     sib1.wait_send()
     sib2.wait_send()
@@ -189,8 +209,8 @@
             scratch_shapes=[
                 pltpu.VMEM((2, D, H), BF16), pltpu.VMEM((2, H, D), BF16),
                 pltpu.VMEM((N, PIECES, CHUNK, DP), BF16), pltpu.VMEM((N, PIECES, CHUNK, DP), BF16),
-                pltpu.VMEM((2, PIECES, CHUNK, DP), BF16), pltpu.VMEM((CHUNK, D), BF16),
-                pltpu.VMEM((CHUNK, 2 * H), BF16),
+                pltpu.VMEM((2, PIECES, CHUNK, DP), BF16), pltpu.VMEM((ROWS, D), BF16),
+                pltpu.VMEM((ROWS, 2 * H), BF16),
                 dma((4,)), dma((2,)), dma((N,)), dma((N,)), dma((N, PIECES)), dma((2, PIECES)),
                 dma((N // 4,)), dma((N // 4,)), dma((N // 4,)),
             ],

time: 478 us -> 418 us (0.87)
  Pallas kernels: 474 us -> 414 us
    pallas_call x1, Pallas kernels: 474 us -> 414 us  [local(): pl.pallas_call(functools.partial(_kernel, S, M, TL), out_shape=jax.ShapeD...]
where the time goes in v2:
time: 418 us; the launch traced here: 417 us
  Pallas kernels  414 us (99%)
    pallas_call x1, Pallas kernels, local(): pl.pallas_call(functools.partial(_kernel, S, M, TL), out_shape=jax.ShapeD...  414 us

profile of v2, /device:TPU:29, one launch (start us, length us, event | category | flops | bytes accessed | tf_op | source)
XLA Modules:
  0.0 416.8 jit_solution(16327048812415465619)
XLA Ops:
  0.0 413.6 %shard_map.46 = bf16[1,4,128,2048]{3,2,1,0:T(8,128)(2,1)} custom-call(bf16[4,128,2048]{2,1,0:T(8,128)(2,1)} %x_ref.1, bf16[1,2,2048]{2,1,0:T(2,128)(2,1)} %g_ref.1, bf16[1,2,2048,2048]{3,2,1,0:T(8,128)(2,1)} %w1_ref.1, bf16[1,2,2048,2048]{3,2,1,0:T(8,128)(2,1)} %w2_ref.1), custom_call_target="tpu_custom_call" | custom-call | tf_op jit(solution)/shard_map/pallas_call | solution.py:203
  413.6 3.2 copy.6

commit v3 on v2

--- a/solution.py
+++ b/solution.py
@@ -11,7 +11,7 @@
 CHUNK = 64
 ROWS = 128
 PIECES = 4
-ORDER = ('A0', 'A1', 'A2', 'A3', 'F0', 'F1', 'F2', 'T0', 'F3', 'T1', 'T2', 'T3')
+ORDER = ('A0', 'A1', 'A2', 'F0', 'F1', 'A3', 'F2', 'F3', 'T0', 'T1', 'T2', 'T3')
 MESH = pl.DeviceIdType.MESH
 F32, BF16 = jnp.float32, jnp.bfloat16
 
@@ -44,8 +44,35 @@
     own1 = pltpu.make_async_copy(w1_ref.at[0, c], W1.at[0], w_sem.at[0])
     own2 = pltpu.make_async_copy(w2_ref.at[0, c], W2.at[0], w_sem.at[2])
     sib1 = remote(w1_ref.at[0, 1 - c], W1.at[1], w_send.at[0], w_sem.at[1], sib)
-    sib2 = remote(w2_ref.at[0, 1 - c], W2.at[1], w_send.at[1], w_sem.at[3], sib)
+    sib2 = [remote(w2_ref.at[0, 1 - c, :, pl.ds(k * DP, DP)], W2.at[1, :, pl.ds(k * DP, DP)],
+                   w_send.at[1 + k], w_sem.at[3 + k], sib) for k in range(PIECES)]
     own1.start()
+    own2.start()
+
+    barrier = pltpu.get_barrier_semaphore()
+
+    def greet(dev):
+        pl.semaphore_signal(barrier, inc=1, device_id=dev, device_id_type=MESH)
+
+    greet(sib)
+    greet(partner)
+
+    @pl.when((c == 0) & (s > 0))
+    def _():
+        greet((s - 1, 2 * xp + 1))
+
+    @pl.when((c == 0) & (s == 0))
+    def _():
+        @pl.loop(1, S)
+        def _(i):
+            greet((i, 2 * (1 - xp)))
+            greet((i, 2 * (1 - xp) + 1))
+
+    pl.semaphore_wait(barrier, 2 + jnp.minimum(s, 1) + c * jnp.minimum(S - 1 - s, 1))
+
+    sib1.start()
+    for cp in sib2:
+        cp.start()
 
     def x_piece(i, k):
         return x_ref.at[i // sub_n, pl.ds(pl.multiple_of((i % sub_n) * C, C), C), pl.ds(k * DP, DP)]
@@ -75,10 +102,6 @@
                 for k in range(PIECES):
                     remote(x_piece(i, k), y.at[4 * i + r, k], in_send.at[i], y_sem.at[4 * i + r],
                            (0, 2 * (1 - xp))).start()
-
-    sib1.start()
-    own2.start()
-    sib2.start()
 
     g = jnp.where(c == 0, g_ref[0, 0:1, :].astype(F32), g_ref[0, 1:2, :].astype(F32))
 
@@ -146,7 +169,8 @@
             else:
                 if first and k == 0:
                     own2.wait()
-                    sib2.wait_recv()
+                if first:
+                    sib2[k].wait_recv()
                 TN = min(512, DP)
                 for j in range(0, DP, TN):
                     o = k * DP + j
@@ -170,7 +194,8 @@
     put_out(N - 1)
 
     sib1.wait_send()
-    sib2.wait_send()
+    for cp in sib2:
+        cp.wait_send()
 
     @pl.when(has_succ)
     def _():
@@ -211,10 +236,10 @@
                 pltpu.VMEM((N, PIECES, CHUNK, DP), BF16), pltpu.VMEM((N, PIECES, CHUNK, DP), BF16),
                 pltpu.VMEM((2, PIECES, CHUNK, DP), BF16), pltpu.VMEM((ROWS, D), BF16),
                 pltpu.VMEM((ROWS, 2 * H), BF16),
-                dma((4,)), dma((2,)), dma((N,)), dma((N,)), dma((N, PIECES)), dma((2, PIECES)),
+                dma((3 + PIECES,)), dma((1 + PIECES,)), dma((N,)), dma((N,)), dma((N, PIECES)), dma((2, PIECES)),
                 dma((N // 4,)), dma((N // 4,)), dma((N // 4,)),
             ],
-            compiler_params=pltpu.CompilerParams(has_side_effects=True, vmem_limit_bytes=67043328),
+            compiler_params=pltpu.CompilerParams(collective_id=0, has_side_effects=True, vmem_limit_bytes=67043328),
         )(x, g, w1, w2)
 
     return jax.shard_map(

time: 418 us -> 408 us (0.976)
  Pallas kernels: 414 us -> 404 us
    pallas_call x1, Pallas kernels: 414 us -> 404 us  [local(): pl.pallas_call(functools.partial(_kernel, S, M, TL), out_shape=jax.ShapeD...]
where the time goes in v3:
time: 408 us
  Pallas kernels  404 us (99%)
    pallas_call x1, Pallas kernels, local(): pl.pallas_call(functools.partial(_kernel, S, M, TL), out_shape=jax.ShapeD...  404 us

profile of v3, /device:TPU:29, one launch (start us, length us, event | category | flops | bytes accessed | tf_op | source)
XLA Modules:
  0.0 407.6 jit_solution(9958029558768178184)
XLA Ops:
  0.0 404.4 %shard_map.46 = bf16[1,4,128,2048]{3,2,1,0:T(8,128)(2,1)} custom-call(bf16[4,128,2048]{2,1,0:T(8,128)(2,1)} %x_ref.1, bf16[1,2,2048]{2,1,0:T(2,128)(2,1)} %g_ref.1, bf16[1,2,2048,2048]{3,2,1,0:T(8,128)(2,1)} %w1_ref.1, bf16[1,2,2048,2048]{3,2,1,0:T(8,128)(2,1)} %w2_ref.1), custom_call_target="tpu_custom_call" | custom-call | tf_op jit(solution)/shard_map/pallas_call | solution.py:228
  404.4 3.2 copy.6

commit v4 on v3

--- a/solution.py
+++ b/solution.py
@@ -113,8 +113,7 @@
         return out_ref.at[0, i // sub_n, pl.ds(pl.multiple_of((i % sub_n) * C, C), C), pl.ds(k * DP, DP)]
 
     def finish(t, k):
-        copy = p_copy(t, k)
-        copy.wait_recv()
+        p_copy(t, k).wait_recv()
         v = y[t, k].astype(F32) + (p[t % 2, k].astype(F32) + xr[t, k].astype(F32))
         y[t, k] = v.astype(BF16)
 
@@ -122,9 +121,9 @@
         def _():
             remote(y.at[t, k], y.at[t, k], y_send.at[t], y_sem.at[t], succ).start()
 
-        copy.wait_send()
-
     def put_out(t):
+        for k in range(PIECES):
+            p_copy(t, k).wait_send()
         mine = (c == 1) & ((t % 4) // 2 == xp)
 
         @pl.when(mine & (t % 2 == 1))

time: 408 us -> 408 us (level)
  no operation moved by 1% of the time
where the time goes in v4:
time: 408 us
  Pallas kernels  404 us (99%)
    pallas_call x1, Pallas kernels, local(): pl.pallas_call(functools.partial(_kernel, S, M, TL), out_shape=jax.ShapeD...  404 us

profile of v4, /device:TPU:29, one launch (start us, length us, event | category | flops | bytes accessed | tf_op | source)
XLA Modules:
  0.0 407.6 jit_solution(14769982536667798162)
XLA Ops:
  0.0 404.4 %shard_map.46 = bf16[1,4,128,2048]{3,2,1,0:T(8,128)(2,1)} custom-call(bf16[4,128,2048]{2,1,0:T(8,128)(2,1)} %x_ref.1, bf16[1,2,2048]{2,1,0:T(2,128)(2,1)} %g_ref.1, bf16[1,2,2048,2048]{3,2,1,0:T(8,128)(2,1)} %w1_ref.1, bf16[1,2,2048,2048]{3,2,1,0:T(8,128)(2,1)} %w2_ref.1), custom_call_target="tpu_custom_call" | custom-call | tf_op jit(solution)/shard_map/pallas_call | solution.py:227
  404.4 3.2 copy.6
